TPU v7x, 32 devices: a whole 2x2x4 slice. The times are simulated.
32 devices in a mesh: section: 4 (over y, x), tp: 8 (over z, core).
Axes of the slice: x: 2, y: 2, z: 4, core: 2. Of those that a mesh axis runs over, the one named last changes fastest.
Arguments:
- grad_in: bfloat16 [4, 128, 4096], P('section', None, 'tp'), may hold values from -6 to 6
- fresh_grads: bfloat16 [1, 128, 4096], P(None, None, 'tp'), may hold values from -6 to 6
- acc_in: float32 [4, 128, 4096], P('section', None, 'tp'), may hold values from -3 to 3
- queries: bfloat16 [4, 2, 128, 4096], P('section', None, None, 'tp'), may hold values from -4.625 to 4.625
- keys: bfloat16 [4, 2, 128, 4096], P('section', None, None, 'tp'), may hold values from -4.625 to 4.625
- values: bfloat16 [4, 2, 128, 4096], P('section', None, None, 'tp'), may hold values from -12 to 12
- query_weight: bfloat16 [4, 4096, 4096], P('section', 'tp'), may hold values from -0.09375 to 0.09375
- key_weight: bfloat16 [4, 4096, 4096], P('section', None, 'tp'), may hold values from -0.125 to 0.125
- value_weight: bfloat16 [4, 4096, 4096], P('section', None, 'tp'), may hold values from -0.125 to 0.125
- out_weight: bfloat16 [4, 4096, 4096], P('section', 'tp'), may hold values from -0.09375 to 0.09375
Outputs:
- grad_out: bfloat16 [4, 128, 4096], P('section', None, 'tp')
- acc_out: float32 [4, 128, 4096], P('section', None, 'tp')
All inputs are finite; a program needn't handle non-finite values.
Results may differ from a plain program's by a relative error of at most 0.025.
Values may be sent and summed in bfloat16 or wider, within the bound.
A program may use at most 64 MiB of HBM per device.

v0:
```python
import jax
import jax.numpy as jnp
from jax import lax
from jax.sharding import PartitionSpec as P

HEAD_DIM = 64
SEQS = 1


def passed_along(value, axis, steps):
    count = lax.axis_size(axis)
    leading, last = (max(0, -steps), min(count, count - steps))
    return lax.ppermute(value, axis, [(source, source + steps) for source in range(leading, last)])


def transpose_product(left, right):
    return lax.dot_general(
        left, right, (((1,), (1,)), ((), ())), preferred_element_type=jnp.float32
    )


def attention_grads(upstream, queries, keys, values):
    token_rows, columns = queries.shape
    enc_rows = keys.shape[0]
    heads = columns // HEAD_DIM
    query_heads = queries.reshape(SEQS, token_rows // SEQS, heads, HEAD_DIM)
    key_heads = keys.reshape(SEQS, enc_rows // SEQS, heads, HEAD_DIM)
    value_heads = values.reshape(SEQS, enc_rows // SEQS, heads, HEAD_DIM)
    upstream_heads = upstream.reshape(SEQS, token_rows // SEQS, heads, HEAD_DIM)
    scores = jnp.einsum(
        "bqhd,bkhd->bhqk", query_heads, key_heads, preferred_element_type=jnp.float32
    )
    attention = jax.nn.softmax(scores, axis=-1)
    weights = attention.astype(jnp.bfloat16)
    output = jnp.einsum("bhqk,bkhd->bqhd", weights, value_heads, preferred_element_type=jnp.float32)
    delta = jnp.sum(upstream_heads.astype(jnp.float32) * output, axis=-1)
    prob_grad = jnp.einsum(
        "bqhd,bkhd->bhqk", upstream_heads, value_heads, preferred_element_type=jnp.float32
    )
    score_grad = (attention * (prob_grad - jnp.transpose(delta, (0, 2, 1))[..., None])).astype(
        jnp.bfloat16
    )
    query_grad = jnp.einsum(
        "bhqk,bkhd->bqhd", score_grad, key_heads, preferred_element_type=jnp.float32
    )
    key_grad = jnp.einsum(
        "bhqk,bqhd->bkhd", score_grad, query_heads, preferred_element_type=jnp.float32
    )
    value_grad = jnp.einsum(
        "bhqk,bqhd->bkhd", weights, upstream_heads, preferred_element_type=jnp.float32
    )
    return (
        query_grad.reshape(token_rows, columns).astype(jnp.bfloat16),
        key_grad.reshape(enc_rows, columns).astype(jnp.bfloat16),
        value_grad.reshape(enc_rows, columns).astype(jnp.bfloat16),
    )


def body(
    grad_in,
    fresh_grads,
    acc_in,
    queries,
    keys,
    values,
    query_weight,
    key_weight,
    value_weight,
    out_weight,
):
    grad_slice = grad_in[0]
    carried = acc_in[0]
    w_query = query_weight[0]
    w_key = key_weight[0]
    w_value = value_weight[0]
    w_out = out_weight[0]
    slot_count = queries.shape[1]
    is_top = lax.axis_index("section") == lax.axis_size("section") - 1
    passed = grad_slice
    for slot in range(slot_count):
        upstream = transpose_product(lax.all_gather(grad_slice, "tp", axis=1, tiled=True), w_out)
        query_grad, key_grad, value_grad = attention_grads(
            upstream.astype(jnp.bfloat16), queries[0, slot], keys[0, slot], values[0, slot]
        )
        branch = transpose_product(lax.all_gather(query_grad, "tp", axis=1, tiled=True), w_query)
        passed = (grad_slice.astype(jnp.float32) + branch).astype(jnp.bfloat16)
        passes_on = slot + 1 < slot_count
        summed = carried
        term = transpose_product(key_grad, w_key) + transpose_product(value_grad, w_value)
        summed = summed + lax.psum_scatter(
            term.astype(jnp.bfloat16), "tp", scatter_dimension=1, tiled=True
        ).astype(jnp.float32)
        if passes_on:
            summed = passed_along(summed.astype(jnp.bfloat16), "section", -1).astype(summed.dtype)
        carried = summed
        if passes_on:
            received = passed_along(passed, "section", -1)
            new_slice = jnp.where(is_top, fresh_grads[slot], received)
            grad_slice = new_slice
            pass
    return (passed[None], carried[None])


def solution(mesh):
    in_specs = (
        P("section", None, "tp"),
        P(None, None, "tp"),
        P("section", None, "tp"),
        P("section", None, None, "tp"),
        P("section", None, None, "tp"),
        P("section", None, None, "tp"),
        P("section", "tp", None),
        P("section", None, "tp"),
        P("section", None, "tp"),
        P("section", "tp", None),
    )
    out_specs = (P("section", None, "tp"), P("section", None, "tp"))
    return jax.shard_map(body, mesh=mesh, in_specs=in_specs, out_specs=out_specs, check_vma=False)
```

profile of v0, /device:TPU:0, one launch (start us, length us, event | category | flops | bytes accessed | tf_op | source)
XLA Modules:
  0.0 196.2 jit_solution(3689854424168437821)
XLA Ops:
  7.2 0.7 all-gather.12.cloned.1.call-update
  7.9 1.0 fusion.55
  8.9 0.1 copy.34
  9.1 1.0 fusion.57
  10.1 0.1 copy.35
  10.2 1.0 fusion.56
  11.2 0.1 copy.37
  11.3 0.4 fusion.58
  11.7 22.9 %all-gather.12.cloned.1.call-done = bf16[1,128,4096]{2,1,0:T(8,128)(2,1)} async-done(((bf16[1,128,512]{2,1,0:T(8,128)(2,1)}), bf16[1,128,4096]{2,1,0:T(8,128)(2,1)}) %all-gather.12.cloned.1.call-update) | async-done | bytes 1048592 | tf_op jit(solution)/shard_map/all_gather | solution.py:81
  34.6 4.0 %fusion.31 = bf16[128,512]{1,0:T(8,128)(2,1)S(1)} fusion(bf16[1,512,4096]{2,1,0:T(8,128)(2,1)} %param.19, bf16[1,128,4096]{2,1,0:T(8,128)(2,1)} %all-gather.12.cloned.1.call-done), kind=kOutput, calls=%fused_computation.35 | convolution fusion | flops 536936448 | bytes 5373952 | tf_op jit(solution)/shard_map/dot_general | solution.py:17
  38.6 0.1 copy.36
  38.7 0.1 copy.38
  38.9 0.2 fusion.40
  39.1 0.3 fusion.25
  39.4 0.9 convolution_convert_fusion.1
  40.3 21.9 %all-gather.6.cloned.1.call-done = bf16[128,4096]{0,1:T(8,128)(2,1)} async-done(((bf16[128,512]{0,1:T(8,128)(2,1)}), bf16[128,4096]{0,1:T(8,128)(2,1)}) %all-gather.6.cloned.1.call-update) | async-done | bytes 1048592 | tf_op jit(solution)/shard_map/all_gather | solution.py:85
  62.3 4.0 %fusion.37 = bf16[128,512]{1,0:T(8,128)(2,1)S(1)} fusion(bf16[128,4096]{0,1:T(8,128)(2,1)} %all-gather.6.cloned.1.call-done, bf16[1,512,4096]{2,1,0:T(8,128)(2,1)} %param.16, bf16[1,128,512]{2,1,0:T(8,128)(2,1)S(1)} %copy-done.3), kind=kOutput, calls=%fused_computation.43 | convolution fusion | flops 537067520 | bytes 5505024 | tf_op jit(solution)/shard_map/dot_general | solution.py:17
  66.3 1.3 collective-permute-start
  67.6 6.2 %collective-permute-done = bf16[128,512]{1,0:T(8,128)(2,1)S(1)} collective-permute-done((bf16[128,512]{1,0:T(8,128)(2,1)S(1)}, bf16[128,512]{1,0:T(8,128)(2,1)S(1)}, u32[]{:S(2)}, u32[]{:S(2)}) %collective-permute-start) | collective-permute-done | bytes 131104 | tf_op jit(solution)/shard_map/ppermute | solution.py:13
  73.8 0.7 bitcast_select_fusion
  74.5 0.0 reduce-scatter.3.cloned.1.call-start
  74.6 0.3 convolution_convert_fusion.5
  74.9 0.3 convolution_convert_fusion.4
  75.2 3.8 %fusion.8 = f32[128,4096]{1,0:T(8,128)S(1)} fusion(bf16[128,512]{0,1:T(8,128)(2,1)S(1)} %bitcast.159, bf16[1,4096,512]{2,1,0:T(8,128)(2,1)} %param.17), kind=kOutput, calls=%fused_computation.10 | convolution fusion | flops 536870912 | bytes 6422528 | tf_op jit(solution)/shard_map/dot_general | solution.py:17
  79.0 2.5 %fusion.2 = bf16[128,4096]{1,0:T(8,128)(2,1)} fusion(f32[128,4096]{1,0:T(8,128)S(1)} %fusion.8, bf16[128,512]{0,1:T(8,128)(2,1)S(1)} %bitcast.165, bf16[1,4096,512]{2,1,0:T(8,128)(2,1)S(1)} %copy-done), kind=kOutput, calls=%fused_computation.4 | convolution fusion | flops 537919488 | bytes 7471104 | tf_op jit(solution)/shard_map/dot_general | solution.py:17
  81.6 0.1 copy.42
  81.7 0.1 copy.43
  81.8 0.1 copy.45
  81.9 0.4 fusion.59
  82.3 14.2 %all-gather.8.cloned.1.call-done = bf16[128,4096]{1,0:T(8,128)(2,1)} async-done(((bf16[128,512]{1,0:T(8,128)(2,1)}), bf16[128,4096]{1,0:T(8,128)(2,1)}) %all-gather.8.cloned.1.call-update) | async-done | bytes 1048592 | tf_op jit(solution)/shard_map/all_gather | solution.py:81
  96.5 4.0 %fusion.34 = bf16[128,512]{1,0:T(8,128)(2,1)S(1)} fusion(bf16[128,4096]{1,0:T(8,128)(2,1)} %all-gather.8.cloned.1.call-done, bf16[1,512,4096]{2,1,0:T(8,128)(2,1)} %param.19), kind=kOutput, calls=%fused_computation.36 | convolution fusion | flops 536936448 | bytes 5373952 | tf_op jit(solution)/shard_map/dot_general | solution.py:17
  100.5 0.1 copy.44
  100.7 0.1 copy.46
  100.8 0.2 fusion.41
  101.0 0.3 fusion.24
  101.3 0.9 convolution_convert_fusion
  102.2 0.0 reduce-scatter.5.cloned.1.call-start
  102.2 0.3 convolution_convert_fusion.3
  102.5 0.3 convolution_convert_fusion.2
  102.8 3.9 %fusion.6 = f32[128,4096]{1,0:T(8,128)S(1)} fusion(bf16[128,512]{0,1:T(8,128)(2,1)S(1)} %bitcast.160, bf16[1,4096,512]{2,1,0:T(8,128)(2,1)} %param.17), kind=kOutput, calls=%fused_computation.8 | convolution fusion | flops 536870912 | bytes 6422528 | tf_op jit(solution)/shard_map/dot_general | solution.py:17
  106.8 2.5 %fusion.3 = bf16[128,4096]{1,0:T(8,128)(2,1)} fusion(f32[128,4096]{1,0:T(8,128)S(1)} %fusion.6, bf16[128,512]{0,1:T(8,128)(2,1)S(1)} %bitcast.166, bf16[1,4096,512]{2,1,0:T(8,128)(2,1)S(1)} %copy-done.1), kind=kOutput, calls=%fused_computation.5 | convolution fusion | flops 537919488 | bytes 7471104 | tf_op jit(solution)/shard_map/dot_general | solution.py:17
  109.3 21.6 %reduce-scatter.3.cloned.1.call-done = bf16[128,512]{1,0:T(8,128)(2,1)} async-done(((bf16[128,4096]{1,0:T(8,128)(2,1)}), bf16[128,512]{1,0:T(8,128)(2,1)}) %reduce-scatter.3.cloned.1.call-update) | async-done | bytes 131088 | tf_op jit(solution)/shard_map/reduce_scatter | solution.py:90
  130.9 0.9 fusion.43
  131.8 1.3 collective-permute-start.1
  133.1 20.2 %all-gather.10.cloned.1.call-done = bf16[128,4096]{0,1:T(8,128)(2,1)} async-done(((bf16[128,512]{0,1:T(8,128)(2,1)}), bf16[128,4096]{0,1:T(8,128)(2,1)}) %all-gather.10.cloned.1.call-update) | async-done | bytes 1048592 | tf_op jit(solution)/shard_map/all_gather | solution.py:85
  153.4 4.7 %fusion.46 = bf16[1,128,512]{2,1,0:T(8,128)(2,1)} fusion(bf16[128,512]{1,0:T(8,128)(2,1)S(1)} %copy-done.2, bf16[128,4096]{0,1:T(8,128)(2,1)} %all-gather.10.cloned.1.call-done, bf16[1,512,4096]{2,1,0:T(8,128)(2,1)} %param.16), kind=kOutput, calls=%fused_computation.55 | convolution fusion | flops 537067520 | bytes 5505024 | tf_op jit(solution)/shard_map/dot_general | solution.py:17
  158.1 29.6 %reduce-scatter.5.cloned.1.call-done = bf16[128,512]{1,0:T(8,128)(2,1)} async-done(((bf16[128,4096]{1,0:T(8,128)(2,1)}), bf16[128,512]{1,0:T(8,128)(2,1)}) %reduce-scatter.5.cloned.1.call-update) | async-done | bytes 131088 | tf_op jit(solution)/shard_map/reduce_scatter | solution.py:90
  187.7 1.6 add_bitcast_fusion
  (22 shorter events, 0.3 us)
Async XLA Ops:
  7.2 27.4 %all-gather.12.cloned.1.call-start = ((), (), s32[]{:S(2)}) async-start(), calls=%async_computation.7 | async-start | bytes 1179648 | tf_op jit(solution)/shard_map/all_gather | solution.py:81
  7.9 54.4 %all-gather.6.cloned.1.call-start = ((), (), s32[]{:S(2)}) async-start(), calls=%async_computation.2 | async-start | bytes 1179648 | tf_op jit(solution)/shard_map/all_gather | solution.py:85
  11.7 50.6 %copy-start.3 = (bf16[1,128,512]{2,1,0:T(8,128)(2,1)S(1)}, bf16[1,128,512]{2,1,0:T(8,128)(2,1)}, u32[]{:S(2)}) copy-start(bf16[1,128,512]{2,1,0:T(8,128)(2,1)} %param.10) | copy-start | bytes 393220
  39.1 34.8 %copy-start.5 = (bf16[1,128,512]{2,1,0:T(8,128)(2,1)S(1)}, bf16[1,128,512]{2,1,0:T(8,128)(2,1)}, u32[]{:S(2)}) copy-start(bf16[1,128,512]{2,1,0:T(8,128)(2,1)} %param.11) | copy-start | bytes 393220
  40.3 56.2 %all-gather.8.cloned.1.call-start = ((), (), s32[]{:S(2)}) async-start(), calls=%async_computation.3 | async-start | bytes 1179648 | tf_op jit(solution)/shard_map/all_gather | solution.py:81
  66.3 7.5 %collective-permute-start = (bf16[128,512]{1,0:T(8,128)(2,1)S(1)}, bf16[128,512]{1,0:T(8,128)(2,1)S(1)}, u32[]{:S(2)}, u32[]{:S(2)}) collective-permute-start(bf16[128,512]{1,0:T(8,128)(2,1)S(1)} %fusion.37), channel_id=1, source_target_pairs={{8,0},{16,8},{24,16},{9,1},{17,9},{25,17},{10,2},{18,10},{26,18},{... | collective-permute-start | bytes 393224 | tf_op jit(solution)/shard_map/ppermute | solution.py:13
  74.5 56.4 %reduce-scatter.3.cloned.1.call-start = ((), (), s32[]{:S(2)}) async-start(), calls=%async_computation.5 | async-start | bytes 1179648 | tf_op jit(solution)/shard_map/reduce_scatter | solution.py:90
  74.9 4.2 %copy-start = (bf16[1,4096,512]{2,1,0:T(8,128)(2,1)S(1)}, bf16[1,4096,512]{2,1,0:T(8,128)(2,1)}, u32[]{:S(2)}) copy-start(bf16[1,4096,512]{2,1,0:T(8,128)(2,1)} %param.18) | copy-start | bytes 12582916
  81.5 71.9 %all-gather.10.cloned.1.call-start = ((), (), s32[]{:S(2)}) async-start(), calls=%async_computation.4 | async-start | bytes 1179648 | tf_op jit(solution)/shard_map/all_gather | solution.py:85
  102.2 85.5 %reduce-scatter.5.cloned.1.call-start = ((), (), s32[]{:S(2)}) async-start(), calls=%async_computation.6 | async-start | bytes 1179648 | tf_op jit(solution)/shard_map/reduce_scatter | solution.py:90
  102.5 4.3 %copy-start.1 = (bf16[1,4096,512]{2,1,0:T(8,128)(2,1)S(1)}, bf16[1,4096,512]{2,1,0:T(8,128)(2,1)}, u32[]{:S(2)}) copy-start(bf16[1,4096,512]{2,1,0:T(8,128)(2,1)} %param.18) | copy-start | bytes 12582916
  106.8 24.1 %copy-start.4 = (f32[1,128,512]{2,1,0:T(8,128)S(1)}, f32[1,128,512]{2,1,0:T(8,128)}, u32[]{:S(2)}) copy-start(f32[1,128,512]{2,1,0:T(8,128)} %param.12) | copy-start | bytes 786436
  106.8 46.6 %copy-start.2 = (bf16[128,512]{1,0:T(8,128)(2,1)S(1)}, bf16[128,512]{1,0:T(8,128)(2,1)}, u32[]{:S(2)}) copy-start(bf16[128,512]{1,0:T(8,128)(2,1)} %bitcast_select_fusion) | copy-start | bytes 393220
  131.8 26.2 %collective-permute-start.1 = (bf16[128,512]{1,0:T(8,128)(2,1)S(1)}, bf16[128,512]{1,0:T(8,128)(2,1)S(1)}, u32[]{:S(2)}, u32[]{:S(2)}) collective-permute-start(bf16[128,512]{1,0:T(8,128)(2,1)S(1)} %fusion.43), channel_id=1, source_target_pairs={{8,0},{16,8},{24,16},{9,1},{17,9},{25,17},{10,2},{18,10},{26,18},{... | collective-permute-start | bytes 393224 | tf_op jit(solution)/shard_map/ppermute | solution.py:13
Sparse Core Ops, SparseCore 0:
  9.6 24.9 all-gather.11
  40.4 21.8 all-gather.5
  74.7 21.7 all-gather.7
  98.6 32.2 reduce-scatter.2
  132.9 20.4 all-gather.9
  155.5 32.1 reduce-scatter.4
where the time goes:
time: 196 us
  waiting for transfers between devices  137 us (70%)
  matrix products  34.1 us (17%)
  between operations  14.3 us (7%)
  local copies, waits for them, and re-layouts  4.18 us (2%)
  other arithmetic  3.24 us (2%)
  starting transfers between devices  2.83 us (1%)
    reduce_scatter x2, waiting for transfers between devices, body(): lax.psum_scatter(term.astype(jnp.bfloat16), 'tp', scatter_dimension=1, ti...  51.2 us
    all_gather x2, waiting for transfers between devices, body(): lax.all_gather(query_grad, 'tp', axis=1, tiled=True)  42.2 us
    all_gather x2, waiting for transfers between devices, body(): lax.all_gather(grad_slice, 'tp', axis=1, tiled=True)  37.1 us
    dot_general x8, matrix products, transpose_product(): lax.dot_general(left, right, (((1,), (1,)), ((), ())), preferred_element_...  29.5 us
    ppermute x2, waiting for transfers between devices, passed_along(): lax.ppermute(value, axis, [(source, source + steps) for source in range(l...  6.21 us
  transfers between devices with their start and end apart: 8, of which 7 were waited for; matrix products, arithmetic and copies ran while one was open for 15% of the time, Pallas kernels for 0%

commit v1 on v0

--- a/solution.py
+++ b/solution.py
@@ -5,6 +5,22 @@
 
 HEAD_DIM = 64
 SEQS = 1
+
+
+def gather_around(x, axis, dim):
+    ways, here, step = (lax.axis_size(axis), lax.axis_index(axis), x.shape[dim])
+    lengths = [n * ways if d == dim else n for d, n in enumerate(x.shape)]
+    full = lax.dynamic_update_slice_in_dim(jnp.zeros(lengths, x.dtype), x, here * step, axis=dim)
+    going_up = going_down = x
+    for far in range(1, ways // 2 + 1):
+        going_up = lax.ppermute(going_up, axis, [(d, (d + 1) % ways) for d in range(ways)])
+        full = lax.dynamic_update_slice_in_dim(full, going_up, (here - far) % ways * step, axis=dim)
+        if 2 * far < ways:
+            going_down = lax.ppermute(going_down, axis, [(d, (d - 1) % ways) for d in range(ways)])
+            full = lax.dynamic_update_slice_in_dim(
+                full, going_down, (here + far) % ways * step, axis=dim
+            )
+    return full
 
 
 def passed_along(value, axis, steps):
@@ -78,7 +94,7 @@
     is_top = lax.axis_index("section") == lax.axis_size("section") - 1
     passed = grad_slice
     for slot in range(slot_count):
-        upstream = transpose_product(lax.all_gather(grad_slice, "tp", axis=1, tiled=True), w_out)
+        upstream = transpose_product(gather_around(grad_slice, "tp", 1), w_out)
         query_grad, key_grad, value_grad = attention_grads(
             upstream.astype(jnp.bfloat16), queries[0, slot], keys[0, slot], values[0, slot]
         )

time: 196 us -> 176 us (0.90)
  waiting for transfers between devices: 137 us -> 95 us
  starting transfers between devices: 2.83 us -> 25.5 us
    all_gather x2 -> x0, waiting for transfers between devices: 37.1 us -> none  [body(): lax.all_gather(grad_slice, 'tp', axis=1, tiled=True)]
    ppermute x0 -> x14, waiting for transfers between devices: none -> 31.6 us  [the longest x8 31.5 us: gather_around(): lax.ppermute(going_up, axis, [(d, (d + 1) % ways) for d in range(ways)])]
    ppermute x0 -> x14, starting transfers between devices: none -> 22.7 us  [the longest x6 22 us: gather_around(): lax.ppermute(going_down, axis, [(d, (d - 1) % ways) for d in range(ways)])]
    reduce_scatter x2, waiting for transfers between devices: 51.2 us -> 29.7 us  [body(): lax.psum_scatter(term.astype(jnp.bfloat16), 'tp', scatter_dimension=1, ti...]
    all_gather x2, waiting for transfers between devices: 42.2 us -> 30 us  [body(): lax.all_gather(query_grad, 'tp', axis=1, tiled=True)]
    ppermute x2, waiting for transfers between devices: 6.21 us -> 3.65 us  [passed_along(): lax.ppermute(value, axis, [(source, source + steps) for source in range(l...]
  transfers between devices with their start and end apart: 8 -> 20, of which waited for: 7 -> 12; matrix products, arithmetic and copies ran while one was open for 15% -> 17% of each run, Pallas kernels for 0% -> 0%
where the time goes in v1:
time: 176 us; the launch traced here: 175 us
  waiting for transfers between devices  95 us (54%)
  matrix products  33.5 us (19%)
  starting transfers between devices  25.5 us (14%)
  between operations  14.2 us (8%)
  local copies, waits for them, and re-layouts  4.55 us (3%)
  other arithmetic  2.61 us (1%)
    ppermute x8, waiting for transfers between devices, gather_around(): lax.ppermute(going_up, axis, [(d, (d + 1) % ways) for d in range(ways)])  31.5 us
    all_gather x2, waiting for transfers between devices, body(): lax.all_gather(query_grad, 'tp', axis=1, tiled=True)  30 us
    reduce_scatter x2, waiting for transfers between devices, body(): lax.psum_scatter(term.astype(jnp.bfloat16), 'tp', scatter_dimension=1, ti...  29.7 us
    dot_general x8, matrix products, transpose_product(): lax.dot_general(left, right, (((1,), (1,)), ((), ())), preferred_element_...  28.9 us
    ppermute x6, starting transfers between devices, gather_around(): lax.ppermute(going_down, axis, [(d, (d - 1) % ways) for d in range(ways)])  22 us
    ppermute x2, waiting for transfers between devices, passed_along(): lax.ppermute(value, axis, [(source, source + steps) for source in range(l...  3.65 us
  transfers between devices with their start and end apart: 20, of which 12 were waited for; matrix products, arithmetic and copies ran while one was open for 17% of the time, Pallas kernels for 0%

profile of v1, /device:TPU:0, one launch (start us, length us, event | category | flops | bytes accessed | tf_op | source)
XLA Modules:
  0.0 175.3 jit_solution(12595333482750577755)
XLA Ops:
  7.2 0.5 collective-permute-start
  7.8 4.1 %collective-permute-start.1 = (bf16[128,512]{1,0:T(8,128)(2,1)}, bf16[128,512]{1,0:T(8,128)(2,1)S(1)}, u32[]{:S(2)}, u32[]{:S(2)}) collective-permute-start(bf16[128,512]{1,0:T(8,128)(2,1)} %bitcast.159), channel_id=1, source_target_pairs={{0,7},{1,0},{2,1},{3,2},{4,3},{5,4},{6,5},{7,6},{8,15},{9,8},{10,9... | collective-permute-start | bytes 393224 | tf_op jit(solution)/shard_map/ppermute | solution.py:19
  11.9 1.0 fusion.54
  12.8 0.1 copy.34
  13.0 1.0 fusion.56
  14.1 1.0 fusion.55
  15.2 0.4 fusion.57
  15.8 3.5 %collective-permute-start.3 = (bf16[128,512]{1,0:T(8,128)(2,1)S(1)}, bf16[128,512]{1,0:T(8,128)(2,1)S(1)}, u32[]{:S(2)}, u32[]{:S(2)}) collective-permute-start(bf16[128,512]{1,0:T(8,128)(2,1)S(1)} %collective-permute-done.1), channel_id=1, source_target_pairs={{0,7},{1,0},{2,1},{3,2},{4,3},{5,4},{6,5},{7,6},{8,15},{9,8},{10,9... | collective-permute-start | bytes 393224 | tf_op jit(solution)/shard_map/ppermute | solution.py:19
  19.4 3.3 %collective-permute-done.2 = bf16[128,512]{1,0:T(8,128)(2,1)S(1)} collective-permute-done((bf16[128,512]{1,0:T(8,128)(2,1)S(1)}, bf16[128,512]{1,0:T(8,128)(2,1)S(1)}, u32[]{:S(2)}, u32[]{:S(2)}) %collective-permute-start.2) | collective-permute-done | bytes 131104 | tf_op jit(solution)/shard_map/ppermute | solution.py:16
  22.8 3.7 %collective-permute-start.5 = (bf16[128,512]{1,0:T(8,128)(2,1)S(1)}, bf16[128,512]{1,0:T(8,128)(2,1)S(1)}, u32[]{:S(2)}, u32[]{:S(2)}) collective-permute-start(bf16[128,512]{1,0:T(8,128)(2,1)S(1)} %collective-permute-done.3), channel_id=1, source_target_pairs={{0,7},{1,0},{2,1},{3,2},{4,3},{5,4},{6,5},{7,6},{8,15},{9,8},{10,9... | collective-permute-start | bytes 393224 | tf_op jit(solution)/shard_map/ppermute | solution.py:19
  26.5 2.7 %collective-permute-done.4 = bf16[128,512]{1,0:T(8,128)(2,1)S(1)} collective-permute-done((bf16[128,512]{1,0:T(8,128)(2,1)S(1)}, bf16[128,512]{1,0:T(8,128)(2,1)S(1)}, u32[]{:S(2)}, u32[]{:S(2)}) %collective-permute-start.4) | collective-permute-done | bytes 131104 | tf_op jit(solution)/shard_map/ppermute | solution.py:16
  29.3 6.1 %collective-permute-done.6 = bf16[128,512]{1,0:T(8,128)(2,1)S(1)} collective-permute-done((bf16[128,512]{1,0:T(8,128)(2,1)S(1)}, bf16[128,512]{1,0:T(8,128)(2,1)S(1)}, u32[]{:S(2)}, u32[]{:S(2)}) %collective-permute-start.6) | collective-permute-done | bytes 131104 | tf_op jit(solution)/shard_map/ppermute | solution.py:16
  35.4 3.8 %fusion.31 = bf16[128,512]{1,0:T(8,128)(2,1)S(1)} fusion(bf16[128,4096]{1,0:T(8,128)(2,1)S(1)} %constant_dynamic-update-slice_fusion.8, bf16[1,512,4096]{2,1,0:T(8,128)(2,1)} %param.19), kind=kOutput, calls=%fused_computation.35 | convolution fusion | flops 536936448 | bytes 5373952 | tf_op jit(solution)/shard_map/dot_general | solution.py:33
  39.4 0.2 fusion.40
  39.7 0.3 fusion.25
  40.0 0.9 convolution_convert_fusion.1
  41.0 0.1 copy.43
  41.2 0.3 convolution_convert_fusion.5
  41.4 0.3 convolution_convert_fusion.4
  41.7 3.7 %fusion.8 = f32[128,4096]{1,0:T(8,128)S(1)} fusion(bf16[128,512]{0,1:T(8,128)(2,1)S(1)} %bitcast.160, bf16[1,4096,512]{2,1,0:T(8,128)(2,1)} %param.17), kind=kOutput, calls=%fused_computation.10 | convolution fusion | flops 536870912 | bytes 6422528 | tf_op jit(solution)/shard_map/dot_general | solution.py:33
  45.4 16.5 %all-gather.3.cloned.1.call-done = bf16[128,4096]{0,1:T(8,128)(2,1)} async-done(((bf16[128,512]{0,1:T(8,128)(2,1)}), bf16[128,4096]{0,1:T(8,128)(2,1)}) %all-gather.3.cloned.1.call-update) | async-done | bytes 1048592 | tf_op jit(solution)/shard_map/all_gather | solution.py:101
  62.0 4.2 %fusion.37 = bf16[128,512]{1,0:T(8,128)(2,1)S(1)} fusion(bf16[128,4096]{0,1:T(8,128)(2,1)} %all-gather.3.cloned.1.call-done, bf16[1,512,4096]{2,1,0:T(8,128)(2,1)} %param.16, bf16[1,128,512]{2,1,0:T(8,128)(2,1)S(1)} %copy-done.2), kind=kOutput, calls=%fused_computation.43 | convolution fusion | flops 537067520 | bytes 5505024 | tf_op jit(solution)/shard_map/dot_general | solution.py:33
  66.2 1.3 collective-permute-start.7
  67.5 2.5 %fusion.2 = bf16[128,4096]{1,0:T(8,128)(2,1)} fusion(f32[128,4096]{1,0:T(8,128)S(1)} %fusion.8, bf16[128,512]{0,1:T(8,128)(2,1)S(1)} %bitcast.166, bf16[1,4096,512]{2,1,0:T(8,128)(2,1)S(1)} %copy-done), kind=kOutput, calls=%fused_computation.4 | convolution fusion | flops 537919488 | bytes 7471104 | tf_op jit(solution)/shard_map/dot_general | solution.py:33
  70.0 3.7 %collective-permute-done.7 = bf16[128,512]{1,0:T(8,128)(2,1)S(1)} collective-permute-done((bf16[128,512]{1,0:T(8,128)(2,1)S(1)}, bf16[128,512]{1,0:T(8,128)(2,1)S(1)}, u32[]{:S(2)}, u32[]{:S(2)}) %collective-permute-start.7) | collective-permute-done | bytes 131104 | tf_op jit(solution)/shard_map/ppermute | solution.py:29
  73.9 3.5 %collective-permute-start.9 = (bf16[128,512]{1,0:T(8,128)(2,1)S(1)}, bf16[128,512]{1,0:T(8,128)(2,1)S(1)}, u32[]{:S(2)}, u32[]{:S(2)}) collective-permute-start(bf16[128,512]{1,0:T(8,128)(2,1)S(1)} %get-tuple-element.3), channel_id=1, source_target_pairs={{0,7},{1,0},{2,1},{3,2},{4,3},{5,4},{6,5},{7,6},{8,15},{9,8},{10,9... | collective-permute-start | bytes 393224 | tf_op jit(solution)/shard_map/ppermute | solution.py:19
  77.4 0.4 fusion.58
  77.8 0.1 copy.45
  77.9 3.1 %collective-permute-done.8 = bf16[128,512]{1,0:T(8,128)(2,1)S(1)} collective-permute-done((bf16[128,512]{1,0:T(8,128)(2,1)S(1)}, bf16[128,512]{1,0:T(8,128)(2,1)S(1)}, u32[]{:S(2)}, u32[]{:S(2)}) %collective-permute-start.8) | collective-permute-done | bytes 131104 | tf_op jit(solution)/shard_map/ppermute | solution.py:16
  81.0 3.6 %collective-permute-start.11 = (bf16[128,512]{1,0:T(8,128)(2,1)S(1)}, bf16[128,512]{1,0:T(8,128)(2,1)S(1)}, u32[]{:S(2)}, u32[]{:S(2)}) collective-permute-start(bf16[128,512]{1,0:T(8,128)(2,1)S(1)} %collective-permute-done.9), channel_id=1, source_target_pairs={{0,7},{1,0},{2,1},{3,2},{4,3},{5,4},{6,5},{7,6},{8,15},{9,8},{10,9... | collective-permute-start | bytes 393224 | tf_op jit(solution)/shard_map/ppermute | solution.py:19
  84.6 5.2 %collective-permute-done.10 = bf16[128,512]{1,0:T(8,128)(2,1)S(1)} collective-permute-done((bf16[128,512]{1,0:T(8,128)(2,1)S(1)}, bf16[128,512]{1,0:T(8,128)(2,1)S(1)}, u32[]{:S(2)}, u32[]{:S(2)}) %collective-permute-start.10) | collective-permute-done | bytes 131104 | tf_op jit(solution)/shard_map/ppermute | solution.py:16
  89.8 3.6 %collective-permute-start.13 = (bf16[128,512]{1,0:T(8,128)(2,1)S(1)}, bf16[128,512]{1,0:T(8,128)(2,1)S(1)}, u32[]{:S(2)}, u32[]{:S(2)}) collective-permute-start(bf16[128,512]{1,0:T(8,128)(2,1)S(1)} %collective-permute-done.11), channel_id=1, source_target_pairs={{0,7},{1,0},{2,1},{3,2},{4,3},{5,4},{6,5},{7,6},{8,15},{9,8},{10,9... | collective-permute-start | bytes 393224 | tf_op jit(solution)/shard_map/ppermute | solution.py:19
  93.5 4.5 %collective-permute-done.12 = bf16[128,512]{1,0:T(8,128)(2,1)S(1)} collective-permute-done((bf16[128,512]{1,0:T(8,128)(2,1)S(1)}, bf16[128,512]{1,0:T(8,128)(2,1)S(1)}, u32[]{:S(2)}, u32[]{:S(2)}) %collective-permute-start.12) | collective-permute-done | bytes 131104 | tf_op jit(solution)/shard_map/ppermute | solution.py:16
  98.0 6.7 %collective-permute-done.14 = bf16[128,512]{1,0:T(8,128)(2,1)S(1)} collective-permute-done((bf16[128,512]{1,0:T(8,128)(2,1)S(1)}, bf16[128,512]{1,0:T(8,128)(2,1)S(1)}, u32[]{:S(2)}, u32[]{:S(2)}) %collective-permute-start.14) | collective-permute-done | bytes 131104 | tf_op jit(solution)/shard_map/ppermute | solution.py:16
  104.6 3.7 %fusion.34 = bf16[128,512]{1,0:T(8,128)(2,1)S(1)} fusion(bf16[128,4096]{1,0:T(8,128)(2,1)S(1)} %constant_dynamic-update-slice_fusion, bf16[1,512,4096]{2,1,0:T(8,128)(2,1)} %param.19), kind=kOutput, calls=%fused_computation.36 | convolution fusion | flops 536936448 | bytes 5373952 | tf_op jit(solution)/shard_map/dot_general | solution.py:33
  108.6 0.2 fusion.41
  108.9 0.3 fusion.24
  109.1 0.9 convolution_convert_fusion
  110.1 0.3 convolution_convert_fusion.3
  110.4 0.3 convolution_convert_fusion.2
  110.7 3.8 %fusion.6 = f32[128,4096]{1,0:T(8,128)S(1)} fusion(bf16[128,512]{0,1:T(8,128)(2,1)S(1)} %bitcast.161, bf16[1,4096,512]{2,1,0:T(8,128)(2,1)} %param.17), kind=kOutput, calls=%fused_computation.8 | convolution fusion | flops 536870912 | bytes 6422528 | tf_op jit(solution)/shard_map/dot_general | solution.py:33
  114.5 2.5 %fusion.3 = bf16[128,4096]{1,0:T(8,128)(2,1)} fusion(f32[128,4096]{1,0:T(8,128)S(1)} %fusion.6, bf16[128,512]{0,1:T(8,128)(2,1)S(1)} %bitcast.167, bf16[1,4096,512]{2,1,0:T(8,128)(2,1)S(1)} %copy-done.1), kind=kOutput, calls=%fused_computation.5 | convolution fusion | flops 537919488 | bytes 7471104 | tf_op jit(solution)/shard_map/dot_general | solution.py:33
  117.1 0.9 fusion.42
  118.0 1.3 collective-permute-start.15
  119.3 13.4 %all-gather.5.cloned.1.call-done = bf16[128,4096]{0,1:T(8,128)(2,1)} async-done(((bf16[128,512]{0,1:T(8,128)(2,1)}), bf16[128,4096]{0,1:T(8,128)(2,1)}) %all-gather.5.cloned.1.call-update) | async-done | bytes 1048592 | tf_op jit(solution)/shard_map/all_gather | solution.py:101
  132.8 4.7 %fusion.45 = bf16[1,128,512]{2,1,0:T(8,128)(2,1)} fusion(bf16[128,512]{1,0:T(8,128)(2,1)S(1)} %get-tuple-element.3, bf16[128,4096]{0,1:T(8,128)(2,1)} %all-gather.5.cloned.1.call-done, bf16[1,512,4096]{2,1,0:T(8,128)(2,1)} %param.16), kind=kOutput, calls=%fused_computation.54 | convolution fusion | flops 537067520 | bytes 5505024 | tf_op jit(solution)/shard_map/dot_general | solution.py:33
  137.5 29.7 %reduce-scatter.5.cloned.1.call-done = bf16[128,512]{1,0:T(8,128)(2,1)} async-done(((bf16[128,4096]{1,0:T(8,128)(2,1)}), bf16[128,512]{1,0:T(8,128)(2,1)}) %reduce-scatter.5.cloned.1.call-update) | async-done | bytes 131088 | tf_op jit(solution)/shard_map/reduce_scatter | solution.py:106
  167.1 1.6 add_bitcast_fusion
  (59 shorter events, 1.8 us)
Async XLA Ops:
  7.2 8.5 %copy-start.2 = (bf16[1,128,512]{2,1,0:T(8,128)(2,1)S(1)}, bf16[1,128,512]{2,1,0:T(8,128)(2,1)}, u32[]{:S(2)}) copy-start(bf16[1,128,512]{2,1,0:T(8,128)(2,1)} %param.10) | copy-start | bytes 393220
  7.2 54.8 %all-gather.3.cloned.1.call-start = ((), (), s32[]{:S(2)}) async-start(), calls=%async_computation.2 | async-start | bytes 1179648 | tf_op jit(solution)/shard_map/all_gather | solution.py:101
  7.2 8.5 %collective-permute-start = (bf16[128,512]{1,0:T(8,128)(2,1)}, bf16[128,512]{1,0:T(8,128)(2,1)S(1)}, u32[]{:S(2)}, u32[]{:S(2)}) collective-permute-start(bf16[128,512]{1,0:T(8,128)(2,1)} %bitcast.158), channel_id=1, source_target_pairs={{0,1},{1,2},{2,3},{3,4},{4,5},{5,6},{6,7},{7,0},{8,9},{9,10},{10,1... | collective-permute-start | bytes 393224 | tf_op jit(solution)/shard_map/ppermute | solution.py:16
  7.8 8.1 %collective-permute-start.1 = (bf16[128,512]{1,0:T(8,128)(2,1)}, bf16[128,512]{1,0:T(8,128)(2,1)S(1)}, u32[]{:S(2)}, u32[]{:S(2)}) collective-permute-start(bf16[128,512]{1,0:T(8,128)(2,1)} %bitcast.159), channel_id=1, source_target_pairs={{0,7},{1,0},{2,1},{3,2},{4,3},{5,4},{6,5},{7,6},{8,15},{9,8},{10,9... | collective-permute-start | bytes 393224 | tf_op jit(solution)/shard_map/ppermute | solution.py:19
  15.8 6.9 %collective-permute-start.2 = (bf16[128,512]{1,0:T(8,128)(2,1)S(1)}, bf16[128,512]{1,0:T(8,128)(2,1)S(1)}, u32[]{:S(2)}, u32[]{:S(2)}) collective-permute-start(bf16[128,512]{1,0:T(8,128)(2,1)S(1)} %collective-permute-done), channel_id=1, source_target_pairs={{0,1},{1,2},{2,3},{3,4},{4,5},{5,6},{6,7},{7,0},{8,9},{9,10},{10,1... | collective-permute-start | bytes 393224 | tf_op jit(solution)/shard_map/ppermute | solution.py:16
  15.8 6.9 %collective-permute-start.3 = (bf16[128,512]{1,0:T(8,128)(2,1)S(1)}, bf16[128,512]{1,0:T(8,128)(2,1)S(1)}, u32[]{:S(2)}, u32[]{:S(2)}) collective-permute-start(bf16[128,512]{1,0:T(8,128)(2,1)S(1)} %collective-permute-done.1), channel_id=1, source_target_pairs={{0,7},{1,0},{2,1},{3,2},{4,3},{5,4},{6,5},{7,6},{8,15},{9,8},{10,9... | collective-permute-start | bytes 393224 | tf_op jit(solution)/shard_map/ppermute | solution.py:19
  22.7 6.6 %collective-permute-start.4 = (bf16[128,512]{1,0:T(8,128)(2,1)S(1)}, bf16[128,512]{1,0:T(8,128)(2,1)S(1)}, u32[]{:S(2)}, u32[]{:S(2)}) collective-permute-start(bf16[128,512]{1,0:T(8,128)(2,1)S(1)} %collective-permute-done.2), channel_id=1, source_target_pairs={{0,1},{1,2},{2,3},{3,4},{4,5},{5,6},{6,7},{7,0},{8,9},{9,10},{10,1... | collective-permute-start | bytes 393224 | tf_op jit(solution)/shard_map/ppermute | solution.py:16
  22.8 6.5 %collective-permute-start.5 = (bf16[128,512]{1,0:T(8,128)(2,1)S(1)}, bf16[128,512]{1,0:T(8,128)(2,1)S(1)}, u32[]{:S(2)}, u32[]{:S(2)}) collective-permute-start(bf16[128,512]{1,0:T(8,128)(2,1)S(1)} %collective-permute-done.3), channel_id=1, source_target_pairs={{0,7},{1,0},{2,1},{3,2},{4,3},{5,4},{6,5},{7,6},{8,15},{9,8},{10,9... | collective-permute-start | bytes 393224 | tf_op jit(solution)/shard_map/ppermute | solution.py:19
  29.2 6.2 %collective-permute-start.6 = (bf16[128,512]{1,0:T(8,128)(2,1)S(1)}, bf16[128,512]{1,0:T(8,128)(2,1)S(1)}, u32[]{:S(2)}, u32[]{:S(2)}) collective-permute-start(bf16[128,512]{1,0:T(8,128)(2,1)S(1)} %collective-permute-done.4), channel_id=1, source_target_pairs={{0,1},{1,2},{2,3},{3,4},{4,5},{5,6},{6,7},{7,0},{8,9},{9,10},{10,1... | collective-permute-start | bytes 393224 | tf_op jit(solution)/shard_map/ppermute | solution.py:16
  40.9 76.2 %reduce-scatter.3.cloned.1.call-start = ((), (), s32[]{:S(2)}) async-start(), calls=%async_computation.4 | async-start | bytes 1179648 | tf_op jit(solution)/shard_map/reduce_scatter | solution.py:106
  62.0 5.5 %copy-start = (bf16[1,4096,512]{2,1,0:T(8,128)(2,1)S(1)}, bf16[1,4096,512]{2,1,0:T(8,128)(2,1)}, u32[]{:S(2)}) copy-start(bf16[1,4096,512]{2,1,0:T(8,128)(2,1)} %param.18) | copy-start | bytes 12582916
  66.2 7.5 %collective-permute-start.7 = (bf16[128,512]{1,0:T(8,128)(2,1)S(1)}, bf16[128,512]{1,0:T(8,128)(2,1)S(1)}, u32[]{:S(2)}, u32[]{:S(2)}) collective-permute-start(bf16[128,512]{1,0:T(8,128)(2,1)S(1)} %fusion.37), channel_id=1, source_target_pairs={{8,0},{16,8},{24,16},{9,1},{17,9},{25,17},{10,2},{18,10},{26,18},{... | collective-permute-start | bytes 393224 | tf_op jit(solution)/shard_map/ppermute | solution.py:29
  67.5 6.3 %copy-start.4 = (bf16[1,128,512]{2,1,0:T(8,128)(2,1)S(1)}, bf16[1,128,512]{2,1,0:T(8,128)(2,1)}, u32[]{:S(2)}) copy-start(bf16[1,128,512]{2,1,0:T(8,128)(2,1)} %param.11) | copy-start | bytes 393220
  70.0 62.8 %all-gather.5.cloned.1.call-start = ((), (), s32[]{:S(2)}) async-start(), calls=%async_computation.3 | async-start | bytes 1179648 | tf_op jit(solution)/shard_map/all_gather | solution.py:101
  73.8 7.1 %collective-permute-start.8 = (bf16[128,512]{1,0:T(8,128)(2,1)S(1)}, bf16[128,512]{1,0:T(8,128)(2,1)S(1)}, u32[]{:S(2)}, u32[]{:S(2)}) collective-permute-start(bf16[128,512]{1,0:T(8,128)(2,1)S(1)} %get-tuple-element.3), channel_id=1, source_target_pairs={{0,1},{1,2},{2,3},{3,4},{4,5},{5,6},{6,7},{7,0},{8,9},{9,10},{10,1... | collective-permute-start | bytes 393224 | tf_op jit(solution)/shard_map/ppermute | solution.py:16
  73.9 7.1 %collective-permute-start.9 = (bf16[128,512]{1,0:T(8,128)(2,1)S(1)}, bf16[128,512]{1,0:T(8,128)(2,1)S(1)}, u32[]{:S(2)}, u32[]{:S(2)}) collective-permute-start(bf16[128,512]{1,0:T(8,128)(2,1)S(1)} %get-tuple-element.3), channel_id=1, source_target_pairs={{0,7},{1,0},{2,1},{3,2},{4,3},{5,4},{6,5},{7,6},{8,15},{9,8},{10,9... | collective-permute-start | bytes 393224 | tf_op jit(solution)/shard_map/ppermute | solution.py:19
  81.0 8.8 %collective-permute-start.10 = (bf16[128,512]{1,0:T(8,128)(2,1)S(1)}, bf16[128,512]{1,0:T(8,128)(2,1)S(1)}, u32[]{:S(2)}, u32[]{:S(2)}) collective-permute-start(bf16[128,512]{1,0:T(8,128)(2,1)S(1)} %collective-permute-done.8), channel_id=1, source_target_pairs={{0,1},{1,2},{2,3},{3,4},{4,5},{5,6},{6,7},{7,0},{8,9},{9,10},{10,1... | collective-permute-start | bytes 393224 | tf_op jit(solution)/shard_map/ppermute | solution.py:16
  81.0 8.8 %collective-permute-start.11 = (bf16[128,512]{1,0:T(8,128)(2,1)S(1)}, bf16[128,512]{1,0:T(8,128)(2,1)S(1)}, u32[]{:S(2)}, u32[]{:S(2)}) collective-permute-start(bf16[128,512]{1,0:T(8,128)(2,1)S(1)} %collective-permute-done.9), channel_id=1, source_target_pairs={{0,7},{1,0},{2,1},{3,2},{4,3},{5,4},{6,5},{7,6},{8,15},{9,8},{10,9... | collective-permute-start | bytes 393224 | tf_op jit(solution)/shard_map/ppermute | solution.py:19
  89.8 8.1 %collective-permute-start.12 = (bf16[128,512]{1,0:T(8,128)(2,1)S(1)}, bf16[128,512]{1,0:T(8,128)(2,1)S(1)}, u32[]{:S(2)}, u32[]{:S(2)}) collective-permute-start(bf16[128,512]{1,0:T(8,128)(2,1)S(1)} %collective-permute-done.10), channel_id=1, source_target_pairs={{0,1},{1,2},{2,3},{3,4},{4,5},{5,6},{6,7},{7,0},{8,9},{9,10},{10,1... | collective-permute-start | bytes 393224 | tf_op jit(solution)/shard_map/ppermute | solution.py:16
  89.8 8.1 %collective-permute-start.13 = (bf16[128,512]{1,0:T(8,128)(2,1)S(1)}, bf16[128,512]{1,0:T(8,128)(2,1)S(1)}, u32[]{:S(2)}, u32[]{:S(2)}) collective-permute-start(bf16[128,512]{1,0:T(8,128)(2,1)S(1)} %collective-permute-done.11), channel_id=1, source_target_pairs={{0,7},{1,0},{2,1},{3,2},{4,3},{5,4},{6,5},{7,6},{8,15},{9,8},{10,9... | collective-permute-start | bytes 393224 | tf_op jit(solution)/shard_map/ppermute | solution.py:19
  97.9 6.7 %collective-permute-start.14 = (bf16[128,512]{1,0:T(8,128)(2,1)S(1)}, bf16[128,512]{1,0:T(8,128)(2,1)S(1)}, u32[]{:S(2)}, u32[]{:S(2)}) collective-permute-start(bf16[128,512]{1,0:T(8,128)(2,1)S(1)} %collective-permute-done.12), channel_id=1, source_target_pairs={{0,1},{1,2},{2,3},{3,4},{4,5},{5,6},{6,7},{7,0},{8,9},{9,10},{10,1... | collective-permute-start | bytes 393224 | tf_op jit(solution)/shard_map/ppermute | solution.py:16
  110.0 57.1 %reduce-scatter.5.cloned.1.call-start = ((), (), s32[]{:S(2)}) async-start(), calls=%async_computation.5 | async-start | bytes 1179648 | tf_op jit(solution)/shard_map/reduce_scatter | solution.py:106
  110.3 4.2 %copy-start.1 = (bf16[1,4096,512]{2,1,0:T(8,128)(2,1)S(1)}, bf16[1,4096,512]{2,1,0:T(8,128)(2,1)}, u32[]{:S(2)}) copy-start(bf16[1,4096,512]{2,1,0:T(8,128)(2,1)} %param.18) | copy-start | bytes 12582916
  114.5 2.6 %copy-start.3 = (f32[1,128,512]{2,1,0:T(8,128)S(1)}, f32[1,128,512]{2,1,0:T(8,128)}, u32[]{:S(2)}) copy-start(f32[1,128,512]{2,1,0:T(8,128)} %param.12) | copy-start | bytes 786436
  118.0 19.4 %collective-permute-start.15 = (bf16[128,512]{1,0:T(8,128)(2,1)S(1)}, bf16[128,512]{1,0:T(8,128)(2,1)S(1)}, u32[]{:S(2)}, u32[]{:S(2)}) collective-permute-start(bf16[128,512]{1,0:T(8,128)(2,1)S(1)} %fusion.42), channel_id=1, source_target_pairs={{8,0},{16,8},{24,16},{9,1},{17,9},{25,17},{10,2},{18,10},{26,18},{... | collective-permute-start | bytes 393224 | tf_op jit(solution)/shard_map/ppermute | solution.py:29
Sparse Core Ops, SparseCore 0:
  41.0 20.9 all-gather.2
  70.1 35.3 reduce-scatter.2
  110.2 22.5 all-gather.4
  134.9 32.2 reduce-scatter.4
